TPU v7x, 256 devices: a 8x8x2 block of a 8x8x16 slice. The times are simulated.
256 devices in a mesh: grp: 2 (over z), tp: 128 (over x, y, core).
Axes of the slice: x: 8, y: 8, z: 2, core: 2. Of those that a mesh axis runs over, the one named last changes fastest.
The devices are a block of a 8x8x16 slice.
Arguments:
- hidden_in: float32 [64, 4608], P('grp'), parts along dimension 0, may hold values from -6 to 6
- prefill_cache: bfloat16 [128, 1, 2, 4, 128, 8, 256], P('tp', None, None, 'grp'), parts along dimension 3, may hold values from -6 to 6
- lengths: int32 [64], P('grp'), parts along dimension 0, may hold values from 1 to 1023
- page_table: int32 [64, 128], P('grp'), parts along dimension 0, may hold values from 0 to 127, each once within a row
- qkv_weight: bfloat16 [1, 8192, 4608], P(None, 'tp'), may hold values from -0.09375 to 0.09375
- out_weight: bfloat16 [1, 4608, 4096], P(None, 'tp'), may hold values from -0.09375 to 0.09375
- gate_up_weight: bfloat16 [1, 2, 18432, 4608], P(None, None, 'tp'), may hold values from -0.09375 to 0.09375
- down_weight: bfloat16 [1, 18432, 4608], P(None, 'tp'), may hold values from -0.15625 to 0.15625
- norm_gains: float32 [1, 4, 4608], replicated, may hold values from 0.25 to 1.75
Outputs:
- hidden_out: float32 [64, 4608], P('grp', 'tp'), parts along dimension 0
- decode_cache: bfloat16 [128, 1, 2, 64, 8, 2048], P('tp', None, None, 'grp'), parts along dimension 3
There are 2 independent parts, one for each index of `grp`. A program takes and returns all parts, laid end to end along the dimension named above; an argument that names none is the same for every part. Nothing has to cross between parts.
Inputs may be any that keep to these rules, and one draw needn't show every extreme that they name: Request r's new token takes position lengths[r]. Each row is a permutation of 0 to 127; page j of request r holds cache positions page_table[r, j] * 8 to page_table[r, j] * 8 + 7.
All inputs are finite; a program needn't handle non-finite values.
Results may differ from a plain program's by a relative error of at most 0.012.
The roundings to bfloat16 on the way count: a program that leaves them out, or rounds other values in their place, can miss the bound.
Values may be sent and summed in bfloat16 or wider, within the bound.
A program may use at most 64 MiB of HBM per device.

v0:
```python
import jax
import jax.numpy as jnp
from jax import lax
from jax.sharding import Mesh
from jax.sharding import PartitionSpec as P

D = 4608
HEADS = 32
KV_HEADS = 16
HEAD_DIM = 128
PREFILL_TP = 8
TP = ("tp_0", "tp_1", "tp_2")
EPSILON = 1e-06
SOFTCAP = 50.0


def cut_along(shard, dim, size):
    before, after = (shard.shape[:dim], shard.shape[dim + 1 :])
    return jnp.moveaxis(shard.reshape(*before, size, -1, *after), dim, 0)


def joined_along(tiles, dim):
    tiles = jnp.moveaxis(tiles, 0, dim)
    shape = tiles.shape
    return tiles.reshape(*shape[:dim], shape[dim] * shape[dim + 1], *shape[dim + 2 :])


def turned_blocks(tiles, axes, turns):
    shape = [lax.axis_size(a) for a in axes]
    tiles = tiles.reshape(*shape, *tiles.shape[1:])
    for k in turns:
        tiles = lax.all_to_all(tiles, axes[k], split_axis=k, concat_axis=k, tiled=True)
    return tiles.reshape(-1, *tiles.shape[len(axes) :])


def exchange_by_chip(shard, groups, turns, split_dim, concat_dim):
    size = lax.axis_size(groups[0]) * lax.axis_size(groups[1])
    tiles = cut_along(shard, split_dim, size)
    return joined_along(turned_blocks(tiles, groups, turns), concat_dim)


def gather_in_order(shard, axes, turns):
    tiles = shard[None]
    for k in turns:
        tiles = lax.all_gather(tiles, axes[k], axis=0, tiled=True)
    held = [lax.axis_size(axes[k]) for k in reversed(turns)]
    tiles = tiles.reshape(*held, *shard.shape)
    turned = sorted(range(len(turns)), key=lambda place: turns[len(turns) - 1 - place])
    return tiles.transpose(*turned, *range(len(turns), tiles.ndim)).reshape(-1, *shard.shape)


def gather_axes(shard, axes, turns, dim):
    return joined_along(gather_in_order(shard, axes, turns), dim)


def own_block(tiles, axes, turns):
    shape = [lax.axis_size(a) for a in axes]
    tiles = tiles.reshape(*shape, *tiles.shape[1:])
    tiles = tiles.transpose(*turns, *range(len(axes), tiles.ndim))
    tiles = tiles.reshape(-1, *tiles.shape[len(axes) :])
    for k in turns:
        tiles = lax.psum_scatter(tiles, axes[k], scatter_dimension=0, tiled=True)
    return tiles[0]


def summed_rows(shard, axes, turns, dim):
    size = lax.axis_size(axes)
    return own_block(cut_along(shard, dim, size), axes, turns)


def one_axis_at_a_time(shard, axes):
    for axis in axes:
        shard = lax.psum(shard, axis)
    return shard


def rms_scale(vector, gain_row):
    meansq = jnp.mean(vector * vector, axis=-1, keepdims=True)
    return vector * lax.rsqrt(meansq + EPSILON) * (1.0 + gain_row)


def rotate(vector, positions):
    half_dim = vector.shape[-1] // 2
    exponent = jnp.arange(half_dim, dtype=jnp.float32) * (-2.0 / vector.shape[-1])
    frequency = jnp.power(jnp.float32(10000.0), exponent)
    angles = positions.astype(jnp.float32)[:, None, None] * frequency
    cosine = jnp.cos(angles)
    sine_term = jnp.sin(angles)
    front_half = vector[..., :half_dim]
    back_half = vector[..., half_dim:]
    return jnp.concatenate(
        [front_half * cosine - back_half * sine_term, back_half * cosine + front_half * sine_term],
        axis=-1,
    )


def capped(raw_scores):
    return SOFTCAP * jnp.tanh(raw_scores / SOFTCAP)


def round_back(vector):
    return lax.optimization_barrier(vector.astype(jnp.bfloat16)).astype(jnp.float32)


def pick_slot(vector, my_group, my_slot):
    inner = lax.dynamic_index_in_dim(vector, my_group, 0, False)
    return lax.dynamic_index_in_dim(inner, my_slot, 1, False)


def take_pages(page_block, page_order):
    return jnp.take(page_block, page_order, axis=2)


def project_rows(left, weight_rows):
    return jnp.einsum("bd,cd->bc", left, weight_rows, preferred_element_type=jnp.float32)


def on_device(
    hidden_in,
    prefill_cache,
    lengths,
    page_table,
    qkv_weight,
    out_weight,
    gate_up_weight,
    down_weight,
    norm_gains,
):
    devices = lax.axis_size(TP)
    my_index = lax.axis_index(TP)
    batch_rows = hidden_in.shape[0]
    groups = devices // PREFILL_TP
    per_group = batch_rows // groups
    local_heads = KV_HEADS // PREFILL_TP
    head_share = HEADS // KV_HEADS
    layer_count = prefill_cache.shape[1]
    page_width = prefill_cache.shape[5]
    score_scale = (D / HEADS) ** (-0.5)
    q_cols = HEADS * HEAD_DIM
    k_cols = KV_HEADS * HEAD_DIM
    my_group = my_index // PREFILL_TP
    my_slot = my_index % PREFILL_TP
    group_rows = lax.dynamic_slice_in_dim(page_table, my_group * per_group, per_group, 0)
    group_lengths = lax.dynamic_slice_in_dim(lengths, my_group * per_group, per_group, 0)
    local_cache = prefill_cache[0]
    page_ids = jnp.arange(devices, dtype=jnp.int32)
    onehot = (group_rows[:, :, None] == page_ids[None, None, :]).astype(jnp.int32)
    inverse = jnp.sum(onehot * page_ids[None, :, None], axis=1)
    arranged = jax.vmap(take_pages, in_axes=(2, 0), out_axes=2)(local_cache, inverse)
    relaid = exchange_by_chip(arranged, (("tp_0", "tp_1"), "tp_2"), (1, 0), 3, 3)
    relaid = relaid.reshape(
        layer_count, 2, per_group, groups, PREFILL_TP, page_width, local_heads, HEAD_DIM
    )
    decode_local = relaid.transpose(0, 1, 3, 2, 5, 4, 6, 7).reshape(
        layer_count, 2, batch_rows, page_width, k_cols
    )
    my_pos = my_index * page_width + jnp.arange(page_width, dtype=jnp.int32)
    fresh_slot = my_pos[None, :] == lengths[:, None]
    kept_cache = local_cache.reshape(
        layer_count, 2, per_group, devices, page_width, local_heads, HEAD_DIM
    )
    cache_pos = (
        group_rows[:, :, None] * page_width + jnp.arange(page_width, dtype=jnp.int32)[None, None, :]
    )
    kept_visible = cache_pos < group_lengths[:, None, None]
    stream = hidden_in
    normed = rms_scale(stream, norm_gains[0, 0]).astype(jnp.bfloat16)
    column_part = project_rows(normed, qkv_weight[0]).astype(jnp.bfloat16)
    projected = gather_axes(column_part, (("tp_0", "tp_1"), "tp_2"), (0, 1), 1)
    queries = rotate(
        projected[:, :q_cols].astype(jnp.float32).reshape(batch_rows, HEADS, HEAD_DIM), lengths
    ).astype(jnp.bfloat16)
    new_key = rotate(
        projected[:, q_cols : q_cols + k_cols]
        .astype(jnp.float32)
        .reshape(batch_rows, KV_HEADS, HEAD_DIM),
        lengths,
    ).astype(jnp.bfloat16)
    new_value = projected[:, q_cols + k_cols :]
    key_layer = jnp.where(
        fresh_slot[:, :, None], new_key.reshape(batch_rows, 1, k_cols), decode_local[0, 0]
    )
    value_layer = jnp.where(
        fresh_slot[:, :, None], new_value.reshape(batch_rows, 1, k_cols), decode_local[0, 1]
    )
    written = [jnp.stack([key_layer, value_layer], axis=0)]
    flat_q = queries.reshape(batch_rows, KV_HEADS, head_share, HEAD_DIM)
    flat_k = new_key.reshape(batch_rows, KV_HEADS, 1, HEAD_DIM)
    flat_v = new_value.reshape(batch_rows, KV_HEADS, 1, HEAD_DIM)
    own_weight = jnp.exp(
        capped(
            jnp.sum(flat_q.astype(jnp.float32) * flat_k.astype(jnp.float32), axis=-1) * score_scale
        )
    )
    own_term = round_back(own_weight)[..., None] * flat_v.astype(jnp.float32)
    shaped_q = flat_q.reshape(groups, per_group, PREFILL_TP, local_heads, head_share, HEAD_DIM)
    shaped_own = own_weight.reshape(groups, per_group, PREFILL_TP, local_heads, head_share)
    shaped_term = own_term.reshape(groups, per_group, PREFILL_TP, local_heads, head_share, HEAD_DIM)
    my_queries = pick_slot(shaped_q, my_group, my_slot)
    cached_keys = kept_cache[0, 0]
    cached_values = kept_cache[0, 1]
    raw_scores = (
        jnp.einsum("ramd,rjcad->ramjc", my_queries, cached_keys, preferred_element_type=jnp.float32)
        * score_scale
    )
    weights = jnp.where(kept_visible[:, None, None, :, :], jnp.exp(capped(raw_scores)), 0.0)
    numerator = jnp.einsum(
        "ramjc,rjcad->ramd",
        weights.astype(jnp.bfloat16),
        cached_values,
        preferred_element_type=jnp.float32,
    )
    numerator = numerator + pick_slot(shaped_term, my_group, my_slot)
    denominator = jnp.sum(weights, axis=(-2, -1)) + pick_slot(shaped_own, my_group, my_slot)
    mine = (
        (numerator / denominator[..., None])
        .astype(jnp.bfloat16)
        .reshape(1, per_group, local_heads * head_share * HEAD_DIM)
    )
    gathered = lax.all_gather(mine, TP, axis=0, tiled=True)
    attended = (
        gathered.reshape(groups, PREFILL_TP, per_group, local_heads * head_share * HEAD_DIM)
        .transpose(0, 2, 1, 3)
        .reshape(batch_rows, q_cols)
    )
    mixed_part = project_rows(attended, out_weight[0]).astype(jnp.bfloat16)
    mixed_out = gather_axes(mixed_part, (("tp_0", "tp_1"), "tp_2"), (0, 1), 1)
    stream = stream + rms_scale(mixed_out.astype(jnp.float32), norm_gains[0, 1])
    ffn_in = rms_scale(stream, norm_gains[0, 2]).astype(jnp.bfloat16)
    gate_proj = project_rows(ffn_in, gate_up_weight[0, 0])
    up_proj = project_rows(ffn_in, gate_up_weight[0, 1])
    active = (jax.nn.gelu(gate_proj, approximate=True) * up_proj).astype(jnp.bfloat16)
    branch = jnp.dot(active, down_weight[0], preferred_element_type=jnp.float32)
    column_count = branch.shape[1] // devices
    portion = summed_rows(branch.astype(jnp.bfloat16), TP, (2, 0, 1), 1).astype(jnp.float32)
    squares = one_axis_at_a_time(jnp.sum(portion * portion, axis=-1), TP)
    gain_part = lax.dynamic_slice_in_dim(norm_gains[0, 3], my_index * column_count, column_count, 0)
    stream_part = lax.dynamic_slice_in_dim(stream, my_index * column_count, column_count, 1)
    result = stream_part + portion * lax.rsqrt(squares[:, None] / D + EPSILON) * (1.0 + gain_part)
    decode_cache = jnp.stack(written, axis=0)[None]
    return (result, decode_cache)


def solution(mesh):
    torus = Mesh(mesh.devices.reshape(mesh.shape["grp"], 8, 8, 2), ("grp", "tp_0", "tp_1", "tp_2"))
    return jax.shard_map(
        on_device,
        mesh=torus,
        in_specs=(
            P("grp", None),
            P(TP, None, None, "grp", None, None, None),
            P("grp"),
            P("grp", None),
            P(None, TP, None),
            P(None, TP, None),
            P(None, None, TP, None),
            P(None, TP, None),
            P(),
        ),
        out_specs=(P("grp", TP), P(TP, None, None, "grp", None, None)),
        check_vma=False,
    )
```

profile of v0, /device:TPU:513, one launch (start us, length us, event | category | flops | bytes accessed | tf_op | source)
XLA Modules:
  0.0 438.4 jit_solution(14225029123569597473)
XLA Ops:
  7.2 0.8 broadcast_multiply_fusion
  8.2 2.8 gather_fusion
  11.5 25.5 %all_to_all.10 = bf16[64,2,1,2,2,1,8,256]{7,6,0,4,3,5,2,1:T(8,128)(2,1)S(1)} all-to-all(bf16[64,2,1,2,2,1,8,256]{7,6,0,4,3,5,2,1:T(8,128)(2,1)S(1)} %copy.124), channel_id=1, replica_groups=mesh['grp'=2,'tp_0'=8,'tp_1'=8,'tp_2'=2] {'tp_2'}, dimensions={1} | all-to-all | bytes 4194304 | tf_op jit(solution)/shard_map/all_to_all | solution.py:32
  37.0 1.6 copy.125
  38.6 7.3 %all-to-all-start.1 = ((bf16[64,2,1,2,2,1,8,256]{7,6,1,4,3,5,2,0:T(8,128)(2,1)}), bf16[64,2,1,2,2,1,8,256]{7,6,1,4,3,5,2,0:T(8,128)(2,1)}, u32[]{:S(2)}, u32[]{:S(2)}) async-start(bf16[64,2,1,2,2,1,8,256]{7,6,1,4,3,5,2,0:T(8,128)(2,1)} %copy.125), calls=%async_computation.4 | async-start | bytes 4194304 | tf_op jit(solution)/shard_map/all_to_all | solution.py:32
  46.1 1.3 add_reduce_fusion
  47.9 83.7 %all-gather = bf16[2048,64]{1,0:T(8,128)(2,1)S(1)} all-gather(bf16[32,64]{1,0:T(8,128)(2,1)S(1)} %convolution_convert_fusion.1), channel_id=2, replica_groups=mesh['grp'=2,'tp_0'=8,'tp_1'=8,'tp_2'=2] {'tp_0','tp_1'}, dimensions={0}, use_global_device_ids=true | all-gather | bytes 266240 | tf_op jit(solution)/shard_map/all_gather | solution.py:45
  131.7 13.7 %all_gather.16 = bf16[128,32,64]{2,1,0:T(8,128)(2,1)S(1)} all-gather(bf16[64,32,64]{2,1,0:T(8,128)(2,1)S(1)} %bitcast.167), channel_id=1, replica_groups=mesh['grp'=2,'tp_0'=8,'tp_1'=8,'tp_2'=2] {'tp_2'}, dimensions={0}, use_global_device_ids=true | all-gather | bytes 786432 | tf_op jit(solution)/shard_map/all_gather | solution.py:45
  145.4 1.1 copy.130
  146.5 1.3 copy.111
  147.9 1.4 copy.112
  149.3 2.9 reshape.346
  152.1 1.8 convert_bitcast_fusion.1
  153.9 1.8 fusion.55
  155.7 1.7 fusion.54
  157.4 1.1 copy.135
  158.5 1.2 reshape.367
  159.7 1.0 copy.136
  161.3 0.8 fusion.53
  162.1 1.3 multiply_reduce_fusion.2
  163.8 2.3 copy.116
  167.0 0.7 constant_dynamic-slice_fusion
  167.7 1.5 fusion.22
  169.2 47.3 %all_gather.17 = bf16[128,2,512]{2,1,0:T(2,128)(2,1)S(1)} all-gather(bf16[1,2,512]{2,1,0:T(2,128)(2,1)S(1)} %reshape.351), channel_id=1, replica_groups=mesh['grp'=2,'tp_0'=8,'tp_1'=8,'tp_2'=2] {'tp_0','tp_1','tp_2'}, dimensions={0}, use_global_device_ids=true | all-gather | bytes 264192 | tf_op jit(solution)/shard_map/all_gather | solution.py:220
  216.9 38.2 %all-gather.1 = bf16[2048,36]{1,0:T(8,128)(2,1)S(1)} all-gather(bf16[32,36]{1,0:T(8,128)(2,1)S(1)} %convolution_convert_fusion.2), channel_id=3, replica_groups=mesh['grp'=2,'tp_0'=8,'tp_1'=8,'tp_2'=2] {'tp_0','tp_1'}, dimensions={0}, use_global_device_ids=true | all-gather | bytes 149760 | tf_op jit(solution)/shard_map/all_gather | solution.py:45
  255.2 14.1 %all_gather.19 = bf16[128,32,36]{2,1,0:T(8,128)(2,1)S(1)} all-gather(bf16[64,32,36]{2,1,0:T(8,128)(2,1)S(1)} %bitcast.168), channel_id=1, replica_groups=mesh['grp'=2,'tp_0'=8,'tp_1'=8,'tp_2'=2] {'tp_2'}, dimensions={0}, use_global_device_ids=true | all-gather | bytes 442368 | tf_op jit(solution)/shard_map/all_gather | solution.py:45
  269.5 2.9 copy.121
  272.5 3.3 reshape.368
  276.2 1.2 multiply_reduce_fusion
  278.1 2.5 convolution_convert_fusion
  280.6 2.8 reshape.355
  283.4 1.6 copy.122
  285.2 16.1 %reduce-scatter.4.cloned.1.call-done = bf16[64,32,36]{2,1,0:T(8,128)(2,1)} async-done(((bf16[128,32,36]{2,1,0:T(8,128)(2,1)}), bf16[64,32,36]{2,1,0:T(8,128)(2,1)}) %reduce-scatter.4.cloned.1.call-update) | async-done | bytes 147472 | tf_op jit(solution)/shard_map/reduce_scatter | solution.py:62
  301.5 0.7 broadcast_compare_fusion
  302.2 35.5 %reduce-scatter.6.cloned.1.call-done = bf16[8,32,36]{2,1,0:T(8,128)(2,1)} async-done(((bf16[64,32,36]{2,1,0:T(8,128)(2,1)}), bf16[8,32,36]{2,1,0:T(8,128)(2,1)}) %reduce-scatter.6.cloned.1.call-update) | async-done | bytes 18448 | tf_op jit(solution)/shard_map/reduce_scatter | solution.py:62
  337.7 0.8 fusion.50
  338.4 0.7 copy.150
  339.1 38.0 %reduce-scatter.8.cloned.1.call-done = bf16[1,32,36]{2,1,0:T(8,128)(2,1)} async-done(((bf16[8,32,36]{2,1,0:T(8,128)(2,1)}), bf16[1,32,36]{2,1,0:T(8,128)(2,1)}) %reduce-scatter.8.cloned.1.call-update) | async-done | bytes 2320 | tf_op jit(solution)/shard_map/reduce_scatter | solution.py:62
  377.2 0.8 fusion.38
  378.0 13.2 %psum.21 = f32[32]{0:T(128)S(1)} all-reduce(f32[32]{0:T(128)S(1)} %fusion.38), channel_id=1, replica_groups=mesh['grp'=2,'tp_0'=8,'tp_1'=8,'tp_2'=2] {'tp_0'}, use_global_device_ids=true, to_apply=%region_9.10 | all-reduce | flops 32 | bytes 256 | tf_op jit(solution)/shard_map/psum | solution.py:73
  391.1 12.0 %psum.22 = f32[32]{0:T(128)S(1)} all-reduce(f32[32]{0:T(128)S(1)} %psum.21), channel_id=1, replica_groups=mesh['grp'=2,'tp_0'=8,'tp_1'=8,'tp_2'=2] {'tp_1'}, use_global_device_ids=true, to_apply=%region_10.11 | all-reduce | flops 32 | bytes 256 | tf_op jit(solution)/shard_map/psum | solution.py:73
  403.1 15.9 %psum.23 = f32[32]{0:T(128)S(1)} all-reduce(f32[32]{0:T(128)S(1)} %psum.22), channel_id=1, replica_groups=mesh['grp'=2,'tp_0'=8,'tp_1'=8,'tp_2'=2] {'tp_2'}, use_global_device_ids=true, to_apply=%region_11.12 | all-reduce | flops 32 | bytes 256 | tf_op jit(solution)/shard_map/psum | solution.py:73
  419.1 1.4 fusion.40
  420.5 1.8 copy.126
  422.2 3.5 copy.127
  425.8 3.3 reshape.361
  429.1 1.2 fusion.24
  430.4 1.5 maximum_bitcast_fusion
  (73 shorter events, 5.3 us)
Async XLA Ops:
  7.2 270.9 %copy-start = (bf16[1,144,4608]{2,1,0:T(8,128)(2,1)S(1)}, bf16[1,144,4608]{2,1,0:T(8,128)(2,1)}, u32[]{:S(2)}) copy-start(bf16[1,144,4608]{2,1,0:T(8,128)(2,1)} %param.16) | copy-start | bytes 3981316
  38.6 7.5 %copy-start.13 = (s32[32]{0:T(128)S(1)}, s32[32]{0:T(128)}, u32[]{:S(2)}) copy-start(s32[32]{0:T(128)} %param.11) | copy-start | bytes 388
  38.6 7.6 %copy-start.12 = (f32[1,4,4608]{2,1,0:T(4,128)S(1)}, f32[1,4,4608]{2,1,0:T(4,128)}, u32[]{:S(2)}) copy-start(f32[1,4,4608]{2,1,0:T(4,128)} %param.17) | copy-start | bytes 221188
  38.6 8.8 %copy-start.2 = (f32[32,4608]{1,0:T(8,128)S(1)}, f32[32,4608]{1,0:T(8,128)}, u32[]{:S(2)}) copy-start(f32[32,4608]{1,0:T(8,128)} %param.9) | copy-start | bytes 1769476
  38.6 9.0 %copy-start.6 = (bf16[1,64,4608]{2,1,0:T(8,128)(2,1)S(1)}, bf16[1,64,4608]{2,1,0:T(8,128)(2,1)}, u32[]{:S(2)}) copy-start(bf16[1,64,4608]{2,1,0:T(8,128)(2,1)} %param.13) | copy-start | bytes 1769476
  38.6 381.9 %all-to-all-start.1 = ((bf16[64,2,1,2,2,1,8,256]{7,6,1,4,3,5,2,0:T(8,128)(2,1)}), bf16[64,2,1,2,2,1,8,256]{7,6,1,4,3,5,2,0:T(8,128)(2,1)}, u32[]{:S(2)}, u32[]{:S(2)}) async-start(bf16[64,2,1,2,2,1,8,256]{7,6,1,4,3,5,2,0:T(8,128)(2,1)} %copy.125), calls=%async_computation.4 | async-start | bytes 4194304 | tf_op jit(solution)/shard_map/all_to_all | solution.py:32
  45.9 255.4 %reduce-scatter.4.cloned.1.call-start = ((), (), s32[]{:S(2)}) async-start(), calls=%async_computation.5 | async-start | bytes 1572864 | tf_op jit(solution)/shard_map/reduce_scatter | solution.py:62
  149.2 6.5 %copy-start.1 = (bf16[1,1,2,2,128,8,256]{6,5,4,3,2,1,0:T(8,128)(2,1)S(1)}, bf16[1,1,2,2,128,8,256]{6,5,4,3,2,1,0:T(8,128)(2,1)}, u32[]{:S(2)}) copy-start(bf16[1,1,2,2,128,8,256]{6,5,4,3,2,1,0:T(8,128)(2,1)} %param.10) | copy-start | bytes 6291460
  161.1 5.4 %copy-start.4 = (bf16[1,1,2,128,8,2,128]{6,4,5,3,2,1,0:T(8,128)(2,1)S(1)}, bf16[1,1,2,128,8,2,128]{6,4,5,3,2,1,0:T(8,128)(2,1)}, u32[]{:S(2)}) copy-start(bf16[1,1,2,128,8,2,128]{6,4,5,3,2,1,0:T(8,128)(2,1)} %get-tuple-element.13) | copy-start | bytes 3145732
  166.5 50.2 %copy-start.9 = (bf16[1,36,4096]{2,1,0:T(8,128)(2,1)S(1)}, bf16[1,36,4096]{2,1,0:T(8,128)(2,1)}, u32[]{:S(2)}) copy-start(bf16[1,36,4096]{2,1,0:T(8,128)(2,1)} %param.14) | copy-start | bytes 884740
  272.5 3.7 copy-start.3
  275.7 1.8 copy-start.5
  275.7 1.8 copy-start.10
  276.2 1.9 copy-start.11
  283.4 18.1 %copy-start.14 = (s32[32]{0:T(128)S(1)}, s32[32]{0:T(128)}, u32[]{:S(2)}) copy-start(s32[32]{0:T(128)} %param.11) | copy-start | bytes 388
  283.4 55.0 %copy-start.8 = (bf16[32,16,128]{2,1,0:T(8,128)(2,1)S(1)}, bf16[32,16,128]{2,1,0:T(8,128)(2,1)}, u32[]{:S(2)}) copy-start(bf16[32,16,128]{2,1,0:T(8,128)(2,1)} %get-tuple-element.8) | copy-start | bytes 393220
  285.1 52.5 %reduce-scatter.6.cloned.1.call-start = ((), (), s32[]{:S(2)}) async-start(), calls=%async_computation.6 | async-start | bytes 589824 | tf_op jit(solution)/shard_map/reduce_scatter | solution.py:62
  301.4 75.7 %reduce-scatter.8.cloned.1.call-start = ((), (), s32[]{:S(2)}) async-start(), calls=%async_computation.7 | async-start | bytes 73728 | tf_op jit(solution)/shard_map/reduce_scatter | solution.py:62
  425.8 3.3 copy-start.7
Sparse Core Ops, SparseCore 0:
  285.3 16.0 reduce-scatter.3
  303.9 33.6 reduce-scatter.5
  340.1 36.9 reduce-scatter.7
where the time goes:
time: 439 us; the launch traced here: 438 us
  blocking collectives  264 us (60%)
  waiting for transfers between devices  89.8 us (20%)
  local copies, waits for them, and re-layouts  40.1 us (9%)
  other arithmetic  17.5 us (4%)
  between operations  14.2 us (3%)
  starting transfers between devices  7.52 us (2%)
  matrix products  5.66 us (1%)
    all_gather x4, blocking collectives, gather_in_order(): tiles = lax.all_gather(tiles, axes[k], axis=0, tiled=True)  150 us
    reduce_scatter x3, waiting for transfers between devices, own_block(): tiles = lax.psum_scatter(tiles, axes[k], scatter_dimension=0, tiled=True)  89.6 us
    all_gather x1, blocking collectives, on_device(): gathered = lax.all_gather(mine, TP, axis=0, tiled=True)  47.3 us
    psum x3, blocking collectives, one_axis_at_a_time(): shard = lax.psum(shard, axis)  41.1 us
    all_to_all x1, blocking collectives, turned_blocks(): lax.all_to_all(tiles, axes[k], split_axis=k, concat_axis=k, tiled=True)  25.5 us
  transfers between devices with their start and end apart: 4, of which 3 were waited for; matrix products, arithmetic and copies ran while one was open for 10% of the time, Pallas kernels for 0%

commit v1 on v0

--- a/solution.py
+++ b/solution.py
@@ -42,7 +42,8 @@
 def gather_in_order(shard, axes, turns):
     tiles = shard[None]
     for k in turns:
-        tiles = lax.all_gather(tiles, axes[k], axis=0, tiled=True)
+        sent = jnp.stack([tiles] * lax.axis_size(axes[k]))
+        tiles = jnp.concatenate(lax.all_to_all(sent, axes[k], 0, 0), axis=0)
     held = [lax.axis_size(axes[k]) for k in reversed(turns)]
     tiles = tiles.reshape(*held, *shard.shape)
     turned = sorted(range(len(turns)), key=lambda place: turns[len(turns) - 1 - place])

time: 439 us -> 392 us (0.89)
  blocking collectives: 264 us -> 109 us
  local copies, waits for them, and re-layouts: 40.1 us -> 76.5 us
  starting transfers between devices: 7.52 us -> 43.7 us
  other arithmetic: 17.5 us -> 31.1 us
  waiting for transfers between devices: 89.8 us -> 103 us
  matrix products: 5.66 us -> 12.6 us
    all_gather x4 -> x0, blocking collectives: 150 us -> none  [gather_in_order(): tiles = lax.all_gather(tiles, axes[k], axis=0, tiled=True)]
    all_to_all x0 -> x2, starting transfers between devices: none -> 32.6 us  [gather_in_order(): tiles = jnp.concatenate(lax.all_to_all(sent, axes[k], 0, 0), axis=0)]
    unnamed x34 -> x32, local copies, waits for them, and re-layouts: 3.03 us -> 18 us
    all_to_all x0 -> x2, waiting for transfers between devices: none -> 10.2 us  [gather_in_order(): tiles = jnp.concatenate(lax.all_to_all(sent, axes[k], 0, 0), axis=0)]
    all_to_all x1 -> x2, blocking collectives: 25.5 us -> 18.1 us  [gather_in_order(): tiles = jnp.concatenate(lax.all_to_all(sent, axes[k], 0, 0), axis=0)]
    convert_element_type x2 -> x3, local copies, waits for them, and re-layouts: 6.21 us -> 11.9 us  [on_device(): stream = stream + rms_scale(mixed_out.astype(jnp.float32), norm_gains[0, 1])]
    all_to_all x1 -> x2, starting transfers between devices: 7.33 us -> 10.7 us  [turned_blocks(): lax.all_to_all(tiles, axes[k], split_axis=k, concat_axis=k, tiled=True)]
  transfers between devices with their start and end apart: 4 -> 7, of which waited for: 3 -> 5; matrix products, arithmetic and copies ran while one was open for 10% -> 25% of each run, Pallas kernels for 0% -> 0%
where the time goes in v1:
time: 392 us; the launch traced here: 390 us
  blocking collectives  109 us (28%)
  waiting for transfers between devices  103 us (26%)
  local copies, waits for them, and re-layouts  76.5 us (20%)
  starting transfers between devices  43.7 us (11%)
  other arithmetic  31.1 us (8%)
  between operations  14.1 us (4%)
  matrix products  12.6 us (3%)
    reduce_scatter x3, waiting for transfers between devices, own_block(): tiles = lax.psum_scatter(tiles, axes[k], scatter_dimension=0, tiled=True)  93.1 us
    all_gather x1, blocking collectives, on_device(): gathered = lax.all_gather(mine, TP, axis=0, tiled=True)  48 us
    psum x3, blocking collectives, one_axis_at_a_time(): shard = lax.psum(shard, axis)  42.6 us
    all_to_all x2, starting transfers between devices, gather_in_order(): tiles = jnp.concatenate(lax.all_to_all(sent, axes[k], 0, 0), axis=0)  32.6 us
    all_to_all x2, blocking collectives, gather_in_order(): tiles = jnp.concatenate(lax.all_to_all(sent, axes[k], 0, 0), axis=0)  18.1 us
    unnamed x32, local copies, waits for them, and re-layouts  18 us
    convert_element_type x3, local copies, waits for them, and re-layouts, on_device(): stream = stream + rms_scale(mixed_out.astype(jnp.float32), norm_gains[0, 1])  11.9 us
    all_to_all x2, starting transfers between devices, turned_blocks(): lax.all_to_all(tiles, axes[k], split_axis=k, concat_axis=k, tiled=True)  10.7 us
  transfers between devices with their start and end apart: 7, of which 5 were waited for; matrix products, arithmetic and copies ran while one was open for 25% of the time, Pallas kernels for 0%

profile of v1, /device:TPU:513, one launch (start us, length us, event | category | flops | bytes accessed | tf_op | source)
XLA Modules:
  0.0 390.1 jit_solution(8180587352634745863)
XLA Ops:
  7.2 2.4 add_reduce_fusion
  10.9 1.6 convolution_convert_fusion.1
  13.3 2.1 reshape.382
  15.4 21.8 %all-to-all-start = ((bf16[64,2,1024]{2,1,0:T(2,128)(2,1)}), bf16[64,2,1024]{2,1,0:T(2,128)(2,1)}, u32[]{:S(2)}, u32[]{:S(2)}) async-start(bf16[64,2,1024]{2,1,0:T(2,128)(2,1)} %reshape.382), calls=%async_computation | async-start | bytes 524288 | tf_op jit(solution)/shard_map/all_to_all | solution.py:46
  38.3 2.5 gather_fusion
  40.7 1.8 broadcast_select_fusion
  45.3 1.7 fusion.54
  50.9 11.4 %all_to_all.30 = bf16[2,2,65536]{2,1,0:T(2,128)(2,1)} all-to-all(bf16[2,2,65536]{2,1,0:T(2,128)(2,1)S(1)} %reshape.384), channel_id=1, replica_groups=mesh['grp'=2,'tp_0'=8,'tp_1'=8,'tp_2'=2] {'tp_2'}, dimensions={0} | all-to-all | bytes 1048576 | tf_op jit(solution)/shard_map/all_to_all | solution.py:46
  62.3 4.1 %all-to-all-start.4 = ((bf16[64,2,1,2,2,1,8,256]{7,6,0,4,3,5,2,1:T(8,128)(2,1)}), bf16[64,2,1,2,2,1,8,256]{7,6,0,4,3,5,2,1:T(8,128)(2,1)S(1)}, u32[]{:S(2)}, u32[]{:S(2)}) async-start(bf16[64,2,1,2,2,1,8,256]{7,6,0,4,3,5,2,1:T(8,128)(2,1)} %copy.151), calls=%async_computation.7 | async-start | bytes 4194304 | tf_op jit(solution)/shard_map/all_to_all | solution.py:32
  66.4 2.5 reshape.385
  71.7 2.7 reshape.343
  75.4 1.8 fusion.55
  78.1 1.9 reshape.363
  83.4 2.1 multiply_reduce_fusion.2
  85.5 1.7 copy.140
  88.6 1.6 reshape.362
  90.1 3.3 copy.141
  95.9 1.6 exp.12
  100.1 1.8 fusion.56
  102.6 2.1 fusion.22
  105.9 48.0 %all_gather.3 = bf16[128,2,512]{2,1,0:T(2,128)(2,1)S(1)} all-gather(bf16[1,2,512]{2,1,0:T(2,128)(2,1)} %reshape.348), channel_id=1, replica_groups=mesh['grp'=2,'tp_0'=8,'tp_1'=8,'tp_2'=2] {'tp_0','tp_1','tp_2'}, dimensions={0}, use_global_device_ids=true | all-gather | bytes 264192 | tf_op jit(solution)/shard_map/all_gather | solution.py:221
  156.1 2.4 reshape.386
  158.6 10.8 %all-to-all-start.2 = ((bf16[64,2,576]{2,1,0:T(2,128)(2,1)}), bf16[64,2,576]{2,1,0:T(2,128)(2,1)}, u32[]{:S(2)}, u32[]{:S(2)}) async-start(bf16[64,2,576]{2,1,0:T(2,128)(2,1)} %reshape.386), calls=%async_computation.2 | async-start | bytes 327680 | tf_op jit(solution)/shard_map/all_to_all | solution.py:46
  169.4 1.6 copy.152
  171.0 8.8 %all-to-all-done.2 = bf16[64,2,576]{2,1,0:T(2,128)(2,1)} async-done(((bf16[64,2,576]{2,1,0:T(2,128)(2,1)}), bf16[64,2,576]{2,1,0:T(2,128)(2,1)}, u32[]{:S(2)}, u32[]{:S(2)}) %all-to-all-start.2) | async-done | bytes 147488 | tf_op jit(solution)/shard_map/all_to_all | solution.py:46
  179.8 1.7 reshape.387
  183.0 6.7 %all_to_all.31 = bf16[2,2,36864]{2,1,0:T(2,128)(2,1)} all-to-all(bf16[2,2,36864]{2,1,0:T(2,128)(2,1)S(1)} %reshape.388), channel_id=1, replica_groups=mesh['grp'=2,'tp_0'=8,'tp_1'=8,'tp_2'=2] {'tp_2'}, dimensions={0} | all-to-all | bytes 589824 | tf_op jit(solution)/shard_map/all_to_all | solution.py:46
  189.7 6.6 %all-to-all-start.5 = ((bf16[64,2,1,2,2,1,8,256]{7,6,1,4,3,5,2,0:T(8,128)(2,1)}), bf16[64,2,1,2,2,1,8,256]{7,6,1,4,3,5,2,0:T(8,128)(2,1)S(1)}, u32[]{:S(2)}, u32[]{:S(2)}) async-start(bf16[64,2,1,2,2,1,8,256]{7,6,1,4,3,5,2,0:T(8,128)(2,1)} %copy.152), calls=%async_computation.8 | async-start | bytes 4194304 | tf_op jit(solution)/shard_map/all_to_all | solution.py:32
  196.3 2.2 reshape.389
  198.5 2.3 convert_bitcast_fusion
  200.8 3.7 copy.147
  204.5 4.1 %copy.148 = f32[32,128,36]{2,1,0:T(8,128)} copy(f32[32,128,36]{2,0,1:T(8,128)} %bitcast.154) | data formatting | bytes 1179648 | tf_op jit(solution)/shard_map/convert_element_type | solution.py:229
  208.6 4.0 %reshape.364 = f32[32,4608]{1,0:T(8,128)} reshape(f32[32,128,36]{2,1,0:T(8,128)} %copy.148) | data formatting | bytes 1179648 | tf_op jit(solution)/shard_map/convert_element_type | solution.py:229
  214.0 1.5 multiply_reduce_fusion
  216.4 2.5 fusion.35
  218.9 3.4 convolution_convert_fusion
  222.3 4.7 %reshape.351 = bf16[32,128,36]{2,1,0:T(8,128)(2,1)} reshape(bf16[32,4608]{1,0:T(8,128)(2,1)} %convolution_convert_fusion) | data formatting | bytes 589824 | tf_op jit(solution)/shard_map/reshape | solution.py:19
  227.0 2.9 copy.149
  230.0 21.9 %reduce-scatter.4.cloned.1.call-done = bf16[64,32,36]{2,1,0:T(8,128)(2,1)} async-done(((bf16[128,32,36]{2,1,0:T(8,128)(2,1)}), bf16[64,32,36]{2,1,0:T(8,128)(2,1)}) %reduce-scatter.4.cloned.1.call-update) | async-done | bytes 147472 | tf_op jit(solution)/shard_map/reduce_scatter | solution.py:63
  253.7 34.5 %reduce-scatter.6.cloned.1.call-done = bf16[8,32,36]{2,1,0:T(8,128)(2,1)} async-done(((bf16[64,32,36]{2,1,0:T(8,128)(2,1)}), bf16[8,32,36]{2,1,0:T(8,128)(2,1)}) %reduce-scatter.6.cloned.1.call-update) | async-done | bytes 18448 | tf_op jit(solution)/shard_map/reduce_scatter | solution.py:63
  289.5 1.6 copy.176
  291.1 36.7 %reduce-scatter.8.cloned.1.call-done = bf16[1,32,36]{2,1,0:T(8,128)(2,1)} async-done(((bf16[8,32,36]{2,1,0:T(8,128)(2,1)}), bf16[1,32,36]{2,1,0:T(8,128)(2,1)}) %reduce-scatter.8.cloned.1.call-update) | async-done | bytes 2320 | tf_op jit(solution)/shard_map/reduce_scatter | solution.py:63
  329.1 13.7 %psum.21 = f32[32]{0:T(128)} all-reduce(f32[32]{0:T(128)} %fusion.38), channel_id=1, replica_groups=mesh['grp'=2,'tp_0'=8,'tp_1'=8,'tp_2'=2] {'tp_0'}, use_global_device_ids=true, to_apply=%region_9.10 | all-reduce | flops 32 | bytes 256 | tf_op jit(solution)/shard_map/psum | solution.py:74
  342.7 12.9 %psum.22 = f32[32]{0:T(128)} all-reduce(f32[32]{0:T(128)} %psum.21), channel_id=1, replica_groups=mesh['grp'=2,'tp_0'=8,'tp_1'=8,'tp_2'=2] {'tp_1'}, use_global_device_ids=true, to_apply=%region_10.11 | all-reduce | flops 32 | bytes 256 | tf_op jit(solution)/shard_map/psum | solution.py:74
  355.7 16.0 %psum.23 = f32[32]{0:T(128)} all-reduce(f32[32]{0:T(128)} %psum.22), channel_id=1, replica_groups=mesh['grp'=2,'tp_0'=8,'tp_1'=8,'tp_2'=2] {'tp_2'}, use_global_device_ids=true, to_apply=%region_11.12 | all-reduce | flops 32 | bytes 256 | tf_op jit(solution)/shard_map/psum | solution.py:74
  373.9 3.5 copy.154
  377.5 3.3 reshape.357
  382.0 1.5 maximum_bitcast_fusion
  (79 shorter events, 40.0 us)
Async XLA Ops:
  7.2 211.7 %copy-start = (bf16[1,144,4608]{2,1,0:T(8,128)(2,1)S(1)}, bf16[1,144,4608]{2,1,0:T(8,128)(2,1)}, u32[]{:S(2)}) copy-start(bf16[1,144,4608]{2,1,0:T(8,128)(2,1)} %param.16) | copy-start | bytes 3981316
  7.2 30.1 %copy-start.9 = (s32[32]{0:T(128)S(1)}, s32[32]{0:T(128)}, u32[]{:S(2)}) copy-start(s32[32]{0:T(128)} %param.11) | copy-start | bytes 388
  7.2 31.0 %copy-start.1 = (bf16[1,1,2,2,128,8,256]{6,5,4,3,2,1,0:T(8,128)(2,1)S(1)}, bf16[1,1,2,2,128,8,256]{6,5,4,3,2,1,0:T(8,128)(2,1)}, u32[]{:S(2)}) copy-start(bf16[1,1,2,2,128,8,256]{6,5,4,3,2,1,0:T(8,128)(2,1)} %param.10) | copy-start | bytes 6291460
  15.4 33.1 %all-to-all-start = ((bf16[64,2,1024]{2,1,0:T(2,128)(2,1)}), bf16[64,2,1024]{2,1,0:T(2,128)(2,1)}, u32[]{:S(2)}, u32[]{:S(2)}) async-start(bf16[64,2,1024]{2,1,0:T(2,128)(2,1)} %reshape.382), calls=%async_computation | async-start | bytes 524288 | tf_op jit(solution)/shard_map/all_to_all | solution.py:46
  62.3 96.3 %all-to-all-start.4 = ((bf16[64,2,1,2,2,1,8,256]{7,6,0,4,3,5,2,1:T(8,128)(2,1)}), bf16[64,2,1,2,2,1,8,256]{7,6,0,4,3,5,2,1:T(8,128)(2,1)S(1)}, u32[]{:S(2)}, u32[]{:S(2)}) async-start(bf16[64,2,1,2,2,1,8,256]{7,6,0,4,3,5,2,1:T(8,128)(2,1)} %copy.151), calls=%async_computation.7 | async-start | bytes 4194304 | tf_op jit(solution)/shard_map/all_to_all | solution.py:32
  80.0 2.5 copy-start.6
  80.0 2.5 copy-start.7
  82.5 1.0 copy-start.3
  82.5 1.0 copy-start.4
  158.6 21.2 %all-to-all-start.2 = ((bf16[64,2,576]{2,1,0:T(2,128)(2,1)}), bf16[64,2,576]{2,1,0:T(2,128)(2,1)}, u32[]{:S(2)}, u32[]{:S(2)}) async-start(bf16[64,2,576]{2,1,0:T(2,128)(2,1)} %reshape.386), calls=%async_computation.2 | async-start | bytes 327680 | tf_op jit(solution)/shard_map/all_to_all | solution.py:46
  189.7 184.1 %all-to-all-start.5 = ((bf16[64,2,1,2,2,1,8,256]{7,6,1,4,3,5,2,0:T(8,128)(2,1)}), bf16[64,2,1,2,2,1,8,256]{7,6,1,4,3,5,2,0:T(8,128)(2,1)S(1)}, u32[]{:S(2)}, u32[]{:S(2)}) async-start(bf16[64,2,1,2,2,1,8,256]{7,6,1,4,3,5,2,0:T(8,128)(2,1)} %copy.152), calls=%async_computation.8 | async-start | bytes 4194304 | tf_op jit(solution)/shard_map/all_to_all | solution.py:32
  196.2 55.7 %reduce-scatter.4.cloned.1.call-start = ((), (), s32[]{:S(2)}) async-start(), calls=%async_computation.9 | async-start | bytes 1572864 | tf_op jit(solution)/shard_map/reduce_scatter | solution.py:63
  212.6 3.7 copy-start.5
  215.5 0.8 copy-start.2
  215.6 0.8 copy-start.8
  230.0 58.2 %reduce-scatter.6.cloned.1.call-start = ((), (), s32[]{:S(2)}) async-start(), calls=%async_computation.10 | async-start | bytes 589824 | tf_op jit(solution)/shard_map/reduce_scatter | solution.py:63
  252.0 75.7 %reduce-scatter.8.cloned.1.call-start = ((), (), s32[]{:S(2)}) async-start(), calls=%async_computation.11 | async-start | bytes 73728 | tf_op jit(solution)/shard_map/reduce_scatter | solution.py:63
Sparse Core Ops, SparseCore 0:
  230.1 21.7 reduce-scatter.3
  254.5 33.6 reduce-scatter.5
  290.7 37.0 reduce-scatter.7
